TPU v7x, 32 devices: a whole 2x2x4 slice. The times are simulated.
32 devices in a mesh: group: 2 (over x), tile: 16 (over z, y, core).
Axes of the slice: x: 2, y: 2, z: 4, core: 2. Of those that a mesh axis runs over, the one named last changes fastest.
Arguments:
- hadamard: int32 [128, 1152], P(None, 'tile'), may hold values from -1 to 1, as said below
- stroke: float32 [2304], P(('group', 'tile')), parts along dimension 0, may hold values from 0.3 to 1
- influence: bfloat16 [3, 2304, 8192], P(None, ('group', 'tile')), parts along dimension 1, may hold values from -0.4375 to 0.4375
- amplitude: float32 [1024, 16, 16], P(('group', 'tile')), parts along dimension 0, may hold values from 0.3 to 1
- aberration: float32 [1024, 16, 16], P(('group', 'tile')), parts along dimension 0, may hold values from -3 to 3
- valid_mask: int32 [1024], P(('group', 'tile')), parts along dimension 0, may hold values from 0 to 1, as said below
Outputs:
- imat: float32 [2304, 2, 512], P(('group', 'tile')), parts along dimension 0
There are 2 independent parts, one for each index of `group`. A program takes and returns all parts, laid end to end along the dimension named above; an argument that names none is the same for every part. Nothing has to cross between parts.
Inputs may be any that keep to these rules, and one draw needn't show every extreme that they name: `hadamard`: each column is one column of a Sylvester-Hadamard matrix whose order is the least power of two not below 1152, restricted to 128 distinct rows of it; different actuators take different columns. `valid_mask`: every pupil tile of 32 subapertures holds at least one valid subaperture.
All inputs are finite; a program needn't handle non-finite values.
Results may differ from a plain program's by a relative error of at most 0.0055.
Values may be sent and summed in bfloat16 or wider, within the bound.
A program may use at most 128 MiB of HBM per device.

v0:
```python
import math
import jax
import jax.numpy as jnp
from jax import lax
from jax.sharding import PartitionSpec as P

PIX = 16
HIGHEST = lax.Precision.HIGHEST


def passed_along(value, axis, steps):
    count = lax.axis_size(axis)
    first, last = (max(0, -steps), min(count, count - steps))
    return lax.ppermute(value, axis, [(source, source + steps) for source in range(first, last)])


def shortened(x):
    return jax.tree.map(lambda a: a.astype(jnp.bfloat16) if a.dtype == jnp.float32 else a, x)


def transform_tables(samples, pixels):
    freqs = jnp.arange(pixels, dtype=jnp.float32) - pixels / 2.0
    places = jnp.arange(samples, dtype=jnp.float32)
    angle = 2.0 * jnp.pi * freqs[:, None] * places[None, :] / (2.0 * samples)
    return (jnp.cos(angle), -jnp.sin(angle))


def kron_tables(samples, pixels):
    table_real, table_imag = transform_tables(samples, pixels)
    kron_real = jnp.kron(table_real, table_real) - jnp.kron(table_imag, table_imag)
    kron_imag = jnp.kron(table_real, table_imag) + jnp.kron(table_imag, table_real)
    upper = jnp.concatenate([kron_real.T, kron_imag.T], axis=1)
    lower = jnp.concatenate([-kron_imag.T, kron_real.T], axis=1)
    transform = jnp.concatenate([upper, lower], axis=0)
    centre = jnp.arange(pixels, dtype=jnp.float32) - (pixels - 1) / 2.0
    along_u = jnp.repeat(centre, pixels)
    along_v = jnp.tile(centre, pixels)
    moments = jnp.stack([jnp.ones_like(along_u), along_u, along_v], axis=1)
    return (transform, moments)


def spot_slopes(phase_map, amplitude, aberration, valid_mask):
    patterns, sub_count, samples = (phase_map.shape[0], phase_map.shape[1], phase_map.shape[2])
    flat = samples * samples
    transform, moments = kron_tables(samples, PIX)
    half = PIX * PIX
    phase_rows = phase_map.reshape(patterns, sub_count, flat)
    amp_rows = amplitude.reshape(sub_count, flat)[None]
    abe_rows = aberration.reshape(sub_count, flat)[None]
    results = []
    for pattern_sign in (1.0, -1.0):
        angles = abe_rows + pattern_sign * phase_rows
        field = jnp.concatenate([amp_rows * jnp.cos(angles), amp_rows * jnp.sin(angles)], axis=2)
        focal = jnp.dot(field.reshape(patterns * sub_count, 2 * flat), transform, precision=HIGHEST)
        intensity = focal[:, :half] * focal[:, :half] + focal[:, half:] * focal[:, half:]
        sums = jnp.dot(intensity, moments, precision=HIGHEST)
        centroid_x = sums[:, 1] / sums[:, 0]
        centroid_y = sums[:, 2] / sums[:, 0]
        results.append(
            jnp.stack([centroid_x, centroid_y], axis=1)
            .reshape(patterns, sub_count, 2)
            .transpose(0, 2, 1)
        )
    weights = valid_mask.astype(jnp.float32)[None, None, :]
    return ((results[0] - results[1]) * 0.5 * weights).astype(jnp.bfloat16)


def shape_term(commands, slab):
    term = jnp.dot(commands, slab, preferred_element_type=jnp.float32).astype(jnp.bfloat16)
    return lax.optimization_barrier(term)


def per_device(hadamard, stroke, influence, amplitude, aberration, valid_mask):
    patterns = hadamard.shape[0]
    sub_count = amplitude.shape[0]
    samples = amplitude.shape[1]
    commands = (stroke[None, :] * hadamard.astype(jnp.float32)).astype(jnp.bfloat16)
    local_term = shape_term(commands, influence[1])
    lower_cmds, lower_slab = passed_along((commands, influence[2]), "tile", 1)
    upper_cmds, upper_slab = passed_along((commands, influence[0]), "tile", -1)
    from_lower = shape_term(lower_cmds, lower_slab)
    from_upper = shape_term(upper_cmds, upper_slab)
    phase_map = (
        local_term.astype(jnp.float32)
        + from_lower.astype(jnp.float32)
        + from_upper.astype(jnp.float32)
    )
    block_rows = math.gcd(patterns, 64)
    blocks = phase_map.reshape(patterns // block_rows, block_rows, sub_count, samples, samples)

    def one_block(pattern_block):
        return spot_slopes(pattern_block, amplitude, aberration, valid_mask)

    slopes = lax.map(one_block, blocks).reshape(patterns, 2, sub_count)
    signs_half = hadamard.astype(jnp.bfloat16)
    summed = jnp.einsum(
        "pa,pcs->acs",
        signs_half,
        lax.all_gather(shortened(slopes), "tile", axis=2, tiled=True),
        preferred_element_type=jnp.float32,
    )
    return summed / (patterns * stroke)[:, None, None]


def solution(mesh):
    placed = (
        P(None, "tile"),
        P(("group", "tile")),
        P(None, ("group", "tile"), None),
        P(("group", "tile"), None, None),
        P(("group", "tile"), None, None),
        P(("group", "tile")),
    )
    return jax.shard_map(
        per_device,
        mesh=mesh,
        in_specs=placed,
        out_specs=P(("group", "tile"), None, None),
        check_vma=False,
    )
```

profile of v0, /device:TPU:0, one launch (start us, length us, event | category | flops | bytes accessed | tf_op | source)
XLA Modules:
  0.0 236.9 jit_solution(5249718799039673560)
XLA Ops:
  0.0 2.8 %slice_bitcast_fusion.1 = (bf16[72,8192]{1,0:T(8,128)(2,1)}, bf16[72,8192]{1,0:T(8,128)(2,1)S(1)}) fusion(bf16[3,72,8192]{2,1,0:T(8,128)(2,1)} %param.10), kind=kLoop, calls=%fused_computation.58 | loop fusion | bytes 4718592 | tf_op jit(solution)/shard_map/squeeze | solution.py:79
  2.8 3.6 %collective-permute-start.1 = (bf16[72,8192]{1,0:T(8,128)(2,1)}, bf16[72,8192]{1,0:T(8,128)(2,1)}, u32[]{:S(2)}, u32[]{:S(2)}) collective-permute-start(bf16[72,8192]{1,0:T(8,128)(2,1)} %get-tuple-element.136), channel_id=1, source_target_pairs={{0,1},{1,2},{2,3},{3,4},{4,5},{5,6},{6,7},{7,8},{8,9},{9,10},{10,1... | collective-permute-start | bytes 3538952 | tf_op jit(solution)/shard_map/ppermute | solution.py:14
  6.4 1.3 collective-permute-start.3
  7.8 4.1 %collective-permute-start = (bf16[128,72]{0,1:T(8,128)(2,1)S(1)}, bf16[128,72]{0,1:T(8,128)(2,1)S(1)}, u32[]{:S(2)}, u32[]{:S(2)}) collective-permute-start(bf16[128,72]{0,1:T(8,128)(2,1)S(1)} %multiply_convert_fusion), channel_id=1, source_target_pairs={{0,1},{1,2},{2,3},{3,4},{4,5},{5,6},{6,7},{7,8},{8,9},{9,10},{10,1... | collective-permute-start | bytes 55304 | tf_op jit(solution)/shard_map/ppermute | solution.py:14
  11.9 1.3 collective-permute-start.2
  13.2 2.0 convolution_convert_fusion.2
  15.3 2.0 convolution_convert_fusion.1
  17.3 2.0 convolution_convert_fusion
  19.3 2.8 %convert_add_fusion = f32[128,8192]{1,0:T(8,128)} fusion(bf16[128,8192]{1,0:T(8,128)(2,1)S(1)} %convolution_convert_fusion, bf16[128,8192]{1,0:T(8,128)(2,1)S(1)} %convolution_convert_fusion.1, bf16[128,8192]{1,0:T(8,128)(2,1)S(1)} %convolution_convert_fusion.2), kind=kLoop, calls=%fused_computation.55 | loop fusion | flops 5242880 | bytes 10485760 | tf_op jit(solution)/shard_map/add | solution.py:84
  22.1 5.6 %copy.28 = f32[128,8192]{0,1:T(8,128)} copy(f32[128,8192]{1,0:T(8,128)} %convert_add_fusion) | data formatting | bytes 8388608 | tf_op jit(solution)/shard_map/add | solution.py:84
  27.7 9.2 %reshape.211 = f32[2,64,32,16,16]{1,0,4,3,2:T(2,128)} reshape(f32[128,8192]{0,1:T(8,128)} %copy.28) | data formatting | bytes 8388608 | tf_op jit(solution)/shard_map/reshape | solution.py:89
  36.9 159.1 %while.12 = (s32[]{:T(128)}, bf16[2,64,2,32]{1,0,3,2:T(2,128)(2,1)S(1)}, f32[32,16,16]{0,2,1:T(8,128)S(1)}, f32[32,16,16]{0,2,1:T(8,128)S(1)}, f32[2,64,32,16,16...) while((s32[]{:T(128)}, ...), condition=%wide.region_1.2_spmd, body=%wide.region_0.1_spmd.sunk | while | flops 12933627904 | bytes 64969588 | solution.py:94
  36.9 9.7 %constant_dynamic-slice_fusion.2 = f32[1,64,32,16,16]{1,0,4,3,2:T(1,128)} fusion(f32[2,64,32,16,16]{1,0,4,3,2:T(2,128)} %get-tuple-element.223, s32[]{:T(128)} %get-tuple-element.209), kind=kLoop, calls=%fused_computation.46.clone.1 | loop fusion | bytes 4194308 | tf_op jit(solution)/shard_map/while/body/jit(dynamic_index_in_dim)/dynamic_slice | solution.py:94
  46.6 12.3 %copy.40 = f32[1,64,32,16,16]{2,1,4,3,0:T(8,128)} copy(f32[1,64,32,16,16]{1,0,4,3,2:T(1,128)} %constant_dynamic-slice_fusion.2) | data formatting | bytes 4194304 | tf_op jit(solution)/shard_map/while/body/jit(dynamic_index_in_dim)/dynamic_slice | solution.py:94
  58.9 7.5 %reshape.239 = f32[2048,256]{0,1:T(8,128)} reshape(f32[1,64,32,16,16]{2,1,4,3,0:T(8,128)} %copy.40) | data formatting | bytes 4194304 | tf_op jit(solution)/shard_map/while/body/eval_jaxpr/reshape | solution.py:47
  66.4 1.9 copy.41
  68.5 16.6 %bitcast_multiply_fusion.5 = (f32[2048,256]{1,0:T(8,128)}, f32[2048,256]{1,0:T(8,128)}, f32[2048,256]{1,0:T(8,128)}, f32[2048,256]{1,0:T(8,128)}) fusion(f32[2048,256]{1,0:T(8,128)S(1)} %copy.41, f32[32,256]{1,0:T(8,128)S(1)} %copy.42, f32[32,256]{1,0:T(8,128)S(1)} %copy.43), kind=kLoop, calls=%fused_computation.3.clone.1 | loop fusion | flops 3670016 | bytes 10551296 | tf_op jit(solution)/shard_map/while/body/eval_jaxpr/mul | solution.py:53
  85.1 0.1 fusion.54
  85.3 2.0 multiply_add_fusion.2
  87.2 2.4 %add.133 = f32[256,256]{1,0:T(8,128)S(1)} reshape(f32[16,16,16,16]{3,2,1,0:T(8,128)} %get-tuple-element.192) | data formatting | bytes 524288 | tf_op jit(solution)/shard_map/while/body/eval_jaxpr/add | solution.py:31
  89.7 0.9 sub.43
  90.7 9.8 %fusion.57 = f32[2048,512]{1,0:T(8,128)} fusion(f32[2048,256]{1,0:T(8,128)} %get-tuple-element.193, f32[2048,256]{1,0:T(8,128)} %get-tuple-element.194, f32[256,256]{0,1:T(8,128)S(1)} %bitcast.82, f32[256,256]{0,1:T(8,128)S(1)} %bitcast_negate_fusion.2, f32[256,256]{0,1:T(8,128)S(1)} %bitcast.80), kind=kOutput, calls=%fused_computation.8.clone.1 | convolution fusion | flops 6444285952 | bytes 9175040 | tf_op jit(solution)/shard_map/while/body/eval_jaxpr/dot_general | solution.py:54
  100.7 4.4 %fusion.58 = f32[2048,3]{0,1:T(4,128)S(1)} fusion(f32[2048,512]{1,0:T(8,128)} %fusion.57, f32[256,1]{0,1:T(1,128)S(1)} %tile.19, f32[256,1]{0,1:T(1,128)S(1)} %reshape.240, f32[3]{0:T(128)S(1)} %pad.6.clone.2), kind=kOutput, calls=%fused_computation.16.clone.1 | convolution fusion | flops 20448768 | bytes 4220940 | tf_op jit(solution)/shard_map/while/body/eval_jaxpr/dot_general | solution.py:56
  105.1 8.5 %fusion.55 = f32[2048,512]{1,0:T(8,128)S(1)} fusion(f32[2048,256]{1,0:T(8,128)} %get-tuple-element.187, f32[2048,256]{1,0:T(8,128)S(1)} %copy-done, f32[256,256]{0,1:T(8,128)S(1)} %bitcast.83, f32[256,256]{0,1:T(8,128)S(1)} %bitcast_negate_fusion.2, f32[256,256]{0,1:T(8,128)S(1)} %bitcast.81), kind=kOutput, calls=%fused_computation.4.clone.1 | convolution fusion | flops 6444285952 | bytes 9175040 | tf_op jit(solution)/shard_map/while/body/eval_jaxpr/dot_general | solution.py:54
  113.6 2.0 fusion.56
  115.7 0.1 fusion.59
  116.1 0.1 copy.44
  116.2 0.2 dynamic_update_slice.8
  116.5 9.7 %constant_dynamic-slice_fusion.2 = f32[1,64,32,16,16]{1,0,4,3,2:T(1,128)} fusion(f32[2,64,32,16,16]{1,0,4,3,2:T(2,128)} %get-tuple-element.223, s32[]{:T(128)} %get-tuple-element.209), kind=kLoop, calls=%fused_computation.46.clone.1 | loop fusion | bytes 4194308 | tf_op jit(solution)/shard_map/while/body/jit(dynamic_index_in_dim)/dynamic_slice | solution.py:94
  126.2 12.3 %copy.40 = f32[1,64,32,16,16]{2,1,4,3,0:T(8,128)} copy(f32[1,64,32,16,16]{1,0,4,3,2:T(1,128)} %constant_dynamic-slice_fusion.2) | data formatting | bytes 4194304 | tf_op jit(solution)/shard_map/while/body/jit(dynamic_index_in_dim)/dynamic_slice | solution.py:94
  138.5 7.5 %reshape.239 = f32[2048,256]{0,1:T(8,128)} reshape(f32[1,64,32,16,16]{2,1,4,3,0:T(8,128)} %copy.40) | data formatting | bytes 4194304 | tf_op jit(solution)/shard_map/while/body/eval_jaxpr/reshape | solution.py:47
  146.0 1.9 copy.41
  148.1 16.6 %bitcast_multiply_fusion.5 = (f32[2048,256]{1,0:T(8,128)}, f32[2048,256]{1,0:T(8,128)}, f32[2048,256]{1,0:T(8,128)}, f32[2048,256]{1,0:T(8,128)}) fusion(f32[2048,256]{1,0:T(8,128)S(1)} %copy.41, f32[32,256]{1,0:T(8,128)S(1)} %copy.42, f32[32,256]{1,0:T(8,128)S(1)} %copy.43), kind=kLoop, calls=%fused_computation.3.clone.1 | loop fusion | flops 3670016 | bytes 10551296 | tf_op jit(solution)/shard_map/while/body/eval_jaxpr/mul | solution.py:53
  164.7 0.1 fusion.54
  164.8 2.0 multiply_add_fusion.2
  166.8 2.4 %add.133 = f32[256,256]{1,0:T(8,128)S(1)} reshape(f32[16,16,16,16]{3,2,1,0:T(8,128)} %get-tuple-element.192) | data formatting | bytes 524288 | tf_op jit(solution)/shard_map/while/body/eval_jaxpr/add | solution.py:31
  169.3 0.9 sub.43
  170.2 9.8 %fusion.57 = f32[2048,512]{1,0:T(8,128)} fusion(f32[2048,256]{1,0:T(8,128)} %get-tuple-element.193, f32[2048,256]{1,0:T(8,128)} %get-tuple-element.194, f32[256,256]{0,1:T(8,128)S(1)} %bitcast.82, f32[256,256]{0,1:T(8,128)S(1)} %bitcast_negate_fusion.2, f32[256,256]{0,1:T(8,128)S(1)} %bitcast.80), kind=kOutput, calls=%fused_computation.8.clone.1 | convolution fusion | flops 6444285952 | bytes 9175040 | tf_op jit(solution)/shard_map/while/body/eval_jaxpr/dot_general | solution.py:54
  180.3 4.4 %fusion.58 = f32[2048,3]{0,1:T(4,128)S(1)} fusion(f32[2048,512]{1,0:T(8,128)} %fusion.57, f32[256,1]{0,1:T(1,128)S(1)} %tile.19, f32[256,1]{0,1:T(1,128)S(1)} %reshape.240, f32[3]{0:T(128)S(1)} %pad.6.clone.2), kind=kOutput, calls=%fused_computation.16.clone.1 | convolution fusion | flops 20448768 | bytes 4220940 | tf_op jit(solution)/shard_map/while/body/eval_jaxpr/dot_general | solution.py:56
  184.7 8.5 %fusion.55 = f32[2048,512]{1,0:T(8,128)S(1)} fusion(f32[2048,256]{1,0:T(8,128)} %get-tuple-element.187, f32[2048,256]{1,0:T(8,128)S(1)} %copy-done, f32[256,256]{0,1:T(8,128)S(1)} %bitcast.83, f32[256,256]{0,1:T(8,128)S(1)} %bitcast_negate_fusion.2, f32[256,256]{0,1:T(8,128)S(1)} %bitcast.81), kind=kOutput, calls=%fused_computation.4.clone.1 | convolution fusion | flops 6444285952 | bytes 9175040 | tf_op jit(solution)/shard_map/while/body/eval_jaxpr/dot_general | solution.py:54
  193.2 2.0 fusion.56
  195.2 0.1 fusion.59
  195.7 0.1 copy.44
  195.8 0.2 dynamic_update_slice.8
  196.0 0.1 reshape.212
  196.1 39.6 %all_gather.3 = bf16[128,2,512]{0,2,1:T(8,128)(2,1)S(1)} all-gather(bf16[128,2,32]{0,2,1:T(8,128)(2,1)S(1)} %reshape.212), channel_id=1, replica_groups=mesh['group'=2,'tile'=16] {'tile'}, dimensions={2}, use_global_device_ids=true | all-gather | bytes 278528 | tf_op jit(solution)/shard_map/all_gather | solution.py:99
  235.7 0.3 fusion.30
  236.0 0.9 copy.31
  (54 shorter events, 1.6 us)
Async XLA Ops:
  0.0 7.7 %copy-start.3 = (s32[128,72]{0,1:T(8,128)S(1)}, s32[128,72]{0,1:T(8,128)}, u32[]{:S(2)}) copy-start(s32[128,72]{0,1:T(8,128)} %param.8) | copy-start | bytes 110596
  0.0 7.7 %copy-start.4 = (f32[72]{0:T(128)S(1)}, f32[72]{0:T(128)}, u32[]{:S(2)}) copy-start(f32[72]{0:T(128)} %param.9) | copy-start | bytes 868
  2.8 12.4 %copy-start.5 = (s32[32]{0:T(128)S(1)}, s32[32]{0:T(128)}, u32[]{:S(2)}) copy-start(s32[32]{0:T(128)} %param.13) | copy-start | bytes 388
  2.8 12.4 %collective-permute-start.1 = (bf16[72,8192]{1,0:T(8,128)(2,1)}, bf16[72,8192]{1,0:T(8,128)(2,1)}, u32[]{:S(2)}, u32[]{:S(2)}) collective-permute-start(bf16[72,8192]{1,0:T(8,128)(2,1)} %get-tuple-element.136), channel_id=1, source_target_pairs={{0,1},{1,2},{2,3},{3,4},{4,5},{5,6},{6,7},{7,8},{8,9},{9,10},{10,1... | collective-permute-start | bytes 3538952 | tf_op jit(solution)/shard_map/ppermute | solution.py:14
  6.4 10.9 %collective-permute-start.3 = (bf16[72,8192]{1,0:T(8,128)(2,1)S(1)}, bf16[72,8192]{1,0:T(8,128)(2,1)}, u32[]{:S(2)}, u32[]{:S(2)}) collective-permute-start(bf16[72,8192]{1,0:T(8,128)(2,1)S(1)} %get-tuple-element.137), channel_id=1, source_target_pairs={{1,0},{2,1},{3,2},{4,3},{5,4},{6,5},{7,6},{8,7},{9,8},{10,9},{11,1... | collective-permute-start | bytes 3538952 | tf_op jit(solution)/shard_map/ppermute | solution.py:14
  7.8 7.5 %collective-permute-start = (bf16[128,72]{0,1:T(8,128)(2,1)S(1)}, bf16[128,72]{0,1:T(8,128)(2,1)S(1)}, u32[]{:S(2)}, u32[]{:S(2)}) collective-permute-start(bf16[128,72]{0,1:T(8,128)(2,1)S(1)} %multiply_convert_fusion), channel_id=1, source_target_pairs={{0,1},{1,2},{2,3},{3,4},{4,5},{5,6},{6,7},{7,8},{8,9},{9,10},{10,1... | collective-permute-start | bytes 55304 | tf_op jit(solution)/shard_map/ppermute | solution.py:14
  11.9 5.4 %collective-permute-start.2 = (bf16[128,72]{0,1:T(8,128)(2,1)S(1)}, bf16[128,72]{0,1:T(8,128)(2,1)S(1)}, u32[]{:S(2)}, u32[]{:S(2)}) collective-permute-start(bf16[128,72]{0,1:T(8,128)(2,1)S(1)} %multiply_convert_fusion), channel_id=1, source_target_pairs={{1,0},{2,1},{3,2},{4,3},{5,4},{6,5},{7,6},{8,7},{9,8},{10,9},{11,1... | collective-permute-start | bytes 55304 | tf_op jit(solution)/shard_map/ppermute | solution.py:14
  27.7 9.2 %copy-start.1 = (f32[32,16,16]{0,2,1:T(8,128)S(1)}, f32[32,16,16]{0,2,1:T(8,128)}, u32[]{:S(2)}) copy-start(f32[32,16,16]{0,2,1:T(8,128)} %param.11) | copy-start | bytes 98308
  27.7 9.2 %copy-start.2 = (f32[32,16,16]{0,2,1:T(8,128)S(1)}, f32[32,16,16]{0,2,1:T(8,128)}, u32[]{:S(2)}) copy-start(f32[32,16,16]{0,2,1:T(8,128)} %param.12) | copy-start | bytes 98308
  100.5 4.7 %copy-start = (f32[2048,256]{1,0:T(8,128)S(1)}, f32[2048,256]{1,0:T(8,128)}, u32[]{:S(2)}) copy-start(f32[2048,256]{1,0:T(8,128)} %get-tuple-element.188) | copy-start | bytes 6291460 | tf_op jit(solution)/shard_map/while
  180.0 4.7 %copy-start = (f32[2048,256]{1,0:T(8,128)S(1)}, f32[2048,256]{1,0:T(8,128)}, u32[]{:S(2)}) copy-start(f32[2048,256]{1,0:T(8,128)} %get-tuple-element.188) | copy-start | bytes 6291460 | tf_op jit(solution)/shard_map/while
where the time goes:
time: 238 us; the launch traced here: 237 us
  local copies, waits for them, and re-layouts  90.3 us (38%)
  matrix products  55.7 us (23%)
  other arithmetic  40.7 us (17%)
  blocking collectives  39.6 us (17%)
  starting transfers between devices  10.3 us (4%)
    dynamic_slice x4, local copies, waits for them, and re-layouts, per_device(): slopes = lax.map(one_block, blocks).reshape(patterns, 2, sub_count)  44.1 us
    all_gather x1, blocking collectives, per_device(): lax.all_gather(shortened(slopes), 'tile', axis=2, tiled=True)  39.6 us
    dot_general x4, matrix products, spot_slopes(): jnp.dot(field.reshape(patterns * sub_count, 2 * flat), transform, precisi...  36.6 us
    mul x2, other arithmetic, spot_slopes(): amp_rows * jnp.cos(angles)  33.3 us
    reshape x4, local copies, waits for them, and re-layouts, spot_slopes(): phase_rows = phase_map.reshape(patterns, sub_count, flat)  18.8 us
    dot_general x4, matrix products, spot_slopes(): sums = jnp.dot(intensity, moments, precision=HIGHEST)  12.9 us
    ppermute x4, starting transfers between devices, passed_along(): lax.ppermute(value, axis, [(source, source + steps) for source in range(f...  10.3 us
    reshape x1, local copies, waits for them, and re-layouts, per_device(): phase_map.reshape(patterns // block_rows, block_rows, sub_count, samples,...  9.2 us
  transfers between devices with their start and end apart: 4, of which 0 were waited for; matrix products, arithmetic and copies ran while one was open for 2% of the time, Pallas kernels for 0%

commit v1 on v0

--- a/solution.py
+++ b/solution.py
@@ -6,6 +6,24 @@
 
 PIX = 16
 HIGHEST = lax.Precision.HIGHEST
+
+
+def collect(value, axis, dim):
+    ways, here, step = (lax.axis_size(axis), lax.axis_index(axis), value.shape[dim])
+    shape = [n * ways if d == dim else n for d, n in enumerate(value.shape)]
+    full = lax.dynamic_update_slice_in_dim(
+        jnp.zeros(shape, value.dtype), value, here * step, axis=dim
+    )
+    going_up = going_down = value
+    for far in range(1, ways // 2 + 1):
+        going_up = lax.ppermute(going_up, axis, [(d, (d + 1) % ways) for d in range(ways)])
+        full = lax.dynamic_update_slice_in_dim(full, going_up, (here - far) % ways * step, axis=dim)
+        if 2 * far < ways:
+            going_down = lax.ppermute(going_down, axis, [(d, (d - 1) % ways) for d in range(ways)])
+            full = lax.dynamic_update_slice_in_dim(
+                full, going_down, (here + far) % ways * step, axis=dim
+            )
+    return full
 
 
 def passed_along(value, axis, steps):
@@ -96,7 +114,7 @@
     summed = jnp.einsum(
         "pa,pcs->acs",
         signs_half,
-        lax.all_gather(shortened(slopes), "tile", axis=2, tiled=True),
+        collect(shortened(slopes), "tile", 2),
         preferred_element_type=jnp.float32,
     )
     return summed / (patterns * stroke)[:, None, None]

time: 238 us -> 287 us (1.21); the launches traced: 237 us -> 282 us
  starting transfers between devices: 10.3 us -> 56.5 us
  blocking collectives: 39.6 us -> 0 us
  loops' own time: 0.19 us -> 16.9 us
  local copies, waits for them, and re-layouts: 90.3 us -> 102 us
  waiting for transfers between devices: 0.01 us -> 8.94 us
    ppermute x0 -> x15, starting transfers between devices: none -> 46.3 us  [the longest x7 24.6 us: collect(): lax.ppermute(going_down, axis, [(d, (d - 1) % ways) for d in range(ways)])]
    all_gather x1 -> x0, blocking collectives: 39.6 us -> none  [per_device(): lax.all_gather(shortened(slopes), 'tile', axis=2, tiled=True)]
    another operation x1, loops' own time: 0.19 us -> 16.9 us  [per_device(): slopes = lax.map(one_block, blocks).reshape(patterns, 2, sub_count)]
    dynamic_update_slice x0 -> x16, local copies, waits for them, and re-layouts: none -> 9.76 us  [the longest x8 4.79 us: collect(): lax.dynamic_update_slice_in_dim(full, going_up, (here - far) % ways * ste...]
    ppermute x0 -> x15, waiting for transfers between devices: none -> 8.93 us  [the longest x8 6.12 us: collect(): lax.ppermute(going_up, axis, [(d, (d + 1) % ways) for d in range(ways)])]
  transfers between devices with their start and end apart: 4 -> 19, of which waited for: 0 -> 12; matrix products, arithmetic and copies ran while one was open for 2% -> 5% of each run, Pallas kernels for 0% -> 0%
where the time goes in v1:
time: 287 us; the launch traced here: 282 us
  local copies, waits for them, and re-layouts  102 us (36%)
  starting transfers between devices  56.5 us (20%)
  matrix products  55.7 us (19%)
  other arithmetic  40.7 us (14%)
  loops' own time  16.9 us (6%)
  waiting for transfers between devices  8.94 us (3%)
    dynamic_slice x4, local copies, waits for them, and re-layouts, per_device(): slopes = lax.map(one_block, blocks).reshape(patterns, 2, sub_count)  44.1 us
    dot_general x4, matrix products, spot_slopes(): jnp.dot(field.reshape(patterns * sub_count, 2 * flat), transform, precisi...  36.6 us
    mul x2, other arithmetic, spot_slopes(): amp_rows * jnp.cos(angles)  33.1 us
    ppermute x7, starting transfers between devices, collect(): lax.ppermute(going_down, axis, [(d, (d - 1) % ways) for d in range(ways)])  24.6 us
    ppermute x8, starting transfers between devices, collect(): lax.ppermute(going_up, axis, [(d, (d + 1) % ways) for d in range(ways)])  21.7 us
    reshape x4, local copies, waits for them, and re-layouts, spot_slopes(): phase_rows = phase_map.reshape(patterns, sub_count, flat)  18.9 us
    another operation x1, loops' own time, per_device(): slopes = lax.map(one_block, blocks).reshape(patterns, 2, sub_count)  16.9 us
    dot_general x4, matrix products, spot_slopes(): sums = jnp.dot(intensity, moments, precision=HIGHEST)  12.9 us
  transfers between devices with their start and end apart: 19, of which 12 were waited for; matrix products, arithmetic and copies ran while one was open for 5% of the time, Pallas kernels for 0%

profile of v1, /device:TPU:0, one launch (start us, length us, event | category | flops | bytes accessed | tf_op | source)
XLA Modules:
  0.0 281.6 jit_solution(12435528621674730928)
XLA Ops:
  0.0 2.9 %slice_bitcast_fusion.1 = (bf16[72,8192]{1,0:T(8,128)(2,1)}, bf16[72,8192]{1,0:T(8,128)(2,1)S(1)}) fusion(bf16[3,72,8192]{2,1,0:T(8,128)(2,1)} %param.10), kind=kLoop, calls=%fused_computation.58 | loop fusion | bytes 4718592 | tf_op jit(solution)/shard_map/squeeze | solution.py:97
  2.9 3.6 %collective-permute-start.1 = (bf16[72,8192]{1,0:T(8,128)(2,1)}, bf16[72,8192]{1,0:T(8,128)(2,1)}, u32[]{:S(2)}, u32[]{:S(2)}) collective-permute-start(bf16[72,8192]{1,0:T(8,128)(2,1)} %get-tuple-element.136), channel_id=1, source_target_pairs={{0,1},{1,2},{2,3},{3,4},{4,5},{5,6},{6,7},{7,8},{8,9},{9,10},{10,1... | collective-permute-start | bytes 3538952 | tf_op jit(solution)/shard_map/ppermute | solution.py:32
  6.4 1.3 collective-permute-start.3
  7.8 4.1 %collective-permute-start = (bf16[128,72]{0,1:T(8,128)(2,1)S(1)}, bf16[128,72]{0,1:T(8,128)(2,1)S(1)}, u32[]{:S(2)}, u32[]{:S(2)}) collective-permute-start(bf16[128,72]{0,1:T(8,128)(2,1)S(1)} %multiply_convert_fusion), channel_id=1, source_target_pairs={{0,1},{1,2},{2,3},{3,4},{4,5},{5,6},{6,7},{7,8},{8,9},{9,10},{10,1... | collective-permute-start | bytes 55304 | tf_op jit(solution)/shard_map/ppermute | solution.py:32
  12.0 1.3 collective-permute-start.2
  13.3 2.0 convolution_convert_fusion.2
  15.3 2.0 convolution_convert_fusion.1
  17.4 2.0 convolution_convert_fusion
  19.4 2.8 convert_add_fusion
  22.2 5.6 %copy.59 = f32[128,8192]{0,1:T(8,128)} copy(f32[128,8192]{1,0:T(8,128)} %convert_add_fusion) | data formatting | bytes 8388608 | tf_op jit(solution)/shard_map/add | solution.py:102
  27.8 9.3 %reshape.211 = f32[2,64,32,16,16]{1,0,4,3,2:T(2,128)} reshape(f32[128,8192]{0,1:T(8,128)} %copy.59) | data formatting | bytes 8388608 | tf_op jit(solution)/shard_map/reshape | solution.py:107
  37.0 175.8 %while.12 = (s32[]{:T(128)}, bf16[2,64,2,32]{1,0,3,2:T(2,128)(2,1)S(1)}, f32[32,16,16]{0,2,1:T(8,128)S(1)}, f32[32,16,16]{0,2,1:T(8,128)S(1)}, f32[2,64,32,16,16...) while((s32[]{:T(128)}, ...), condition=%wide.region_1.2_spmd, body=%wide.region_0.1_spmd.sunk | while | flops 12933627904 | bytes 64969588 | solution.py:112
  53.5 9.7 %constant_dynamic-slice_fusion.2 = f32[1,64,32,16,16]{1,0,4,3,2:T(1,128)} fusion(f32[2,64,32,16,16]{1,0,4,3,2:T(2,128)} %get-tuple-element.223, s32[]{:T(128)} %get-tuple-element.209), kind=kLoop, calls=%fused_computation.46.clone.1 | loop fusion | bytes 4194308 | tf_op jit(solution)/shard_map/while/body/jit(dynamic_index_in_dim)/dynamic_slice | solution.py:112
  63.3 12.3 %copy.87 = f32[1,64,32,16,16]{2,1,4,3,0:T(8,128)} copy(f32[1,64,32,16,16]{1,0,4,3,2:T(1,128)} %constant_dynamic-slice_fusion.2) | data formatting | bytes 4194304 | tf_op jit(solution)/shard_map/while/body/jit(dynamic_index_in_dim)/dynamic_slice | solution.py:112
  75.6 7.5 %reshape.239 = f32[2048,256]{0,1:T(8,128)} reshape(f32[1,64,32,16,16]{2,1,4,3,0:T(8,128)} %copy.87) | data formatting | bytes 4194304 | tf_op jit(solution)/shard_map/while/body/eval_jaxpr/reshape | solution.py:65
  83.1 1.9 copy.88
  85.1 16.6 %bitcast_multiply_fusion.5 = (f32[2048,256]{1,0:T(8,128)}, f32[2048,256]{1,0:T(8,128)}, f32[2048,256]{1,0:T(8,128)}, f32[2048,256]{1,0:T(8,128)}) fusion(f32[2048,256]{1,0:T(8,128)S(1)} %copy.88, f32[32,256]{1,0:T(8,128)S(1)} %copy.89, f32[32,256]{1,0:T(8,128)S(1)} %copy.90), kind=kLoop, calls=%fused_computation.3.clone.1 | loop fusion | flops 3670016 | bytes 10551296 | tf_op jit(solution)/shard_map/while/body/eval_jaxpr/mul | solution.py:71
  101.8 2.0 multiply_add_fusion.2
  103.9 2.4 add.294
  106.3 0.9 sub.75
  107.3 9.8 %fusion.57 = f32[2048,512]{1,0:T(8,128)} fusion(f32[2048,256]{1,0:T(8,128)} %get-tuple-element.193, f32[2048,256]{1,0:T(8,128)} %get-tuple-element.194, f32[256,256]{0,1:T(8,128)S(1)} %bitcast.82, f32[256,256]{0,1:T(8,128)S(1)} %bitcast_negate_fusion.2, f32[256,256]{0,1:T(8,128)S(1)} %bitcast.80), kind=kOutput, calls=%fused_computation.8.clone.1 | convolution fusion | flops 6444285952 | bytes 9175040 | tf_op jit(solution)/shard_map/while/body/eval_jaxpr/dot_general | solution.py:72
  117.4 4.4 %fusion.58 = f32[2048,3]{0,1:T(4,128)S(1)} fusion(f32[2048,512]{1,0:T(8,128)} %fusion.57, f32[256,1]{0,1:T(1,128)S(1)} %tile.19, f32[256,1]{0,1:T(1,128)S(1)} %reshape.240, f32[3]{0:T(128)S(1)} %pad.6.clone.2), kind=kOutput, calls=%fused_computation.16.clone.1 | convolution fusion | flops 20448768 | bytes 4220940 | tf_op jit(solution)/shard_map/while/body/eval_jaxpr/dot_general | solution.py:74
  121.8 8.5 %fusion.55 = f32[2048,512]{1,0:T(8,128)S(1)} fusion(f32[2048,256]{1,0:T(8,128)} %get-tuple-element.187, f32[2048,256]{1,0:T(8,128)S(1)} %copy-done, f32[256,256]{0,1:T(8,128)S(1)} %bitcast.83, f32[256,256]{0,1:T(8,128)S(1)} %bitcast_negate_fusion.2, f32[256,256]{0,1:T(8,128)S(1)} %bitcast.81), kind=kOutput, calls=%fused_computation.4.clone.1 | convolution fusion | flops 6444285952 | bytes 9175040 | tf_op jit(solution)/shard_map/while/body/eval_jaxpr/dot_general | solution.py:72
  130.3 2.0 fusion.56
  133.1 9.7 %constant_dynamic-slice_fusion.2 = f32[1,64,32,16,16]{1,0,4,3,2:T(1,128)} fusion(f32[2,64,32,16,16]{1,0,4,3,2:T(2,128)} %get-tuple-element.223, s32[]{:T(128)} %get-tuple-element.209), kind=kLoop, calls=%fused_computation.46.clone.1 | loop fusion | bytes 4194308 | tf_op jit(solution)/shard_map/while/body/jit(dynamic_index_in_dim)/dynamic_slice | solution.py:112
  142.8 12.3 %copy.87 = f32[1,64,32,16,16]{2,1,4,3,0:T(8,128)} copy(f32[1,64,32,16,16]{1,0,4,3,2:T(1,128)} %constant_dynamic-slice_fusion.2) | data formatting | bytes 4194304 | tf_op jit(solution)/shard_map/while/body/jit(dynamic_index_in_dim)/dynamic_slice | solution.py:112
  155.1 7.5 %reshape.239 = f32[2048,256]{0,1:T(8,128)} reshape(f32[1,64,32,16,16]{2,1,4,3,0:T(8,128)} %copy.87) | data formatting | bytes 4194304 | tf_op jit(solution)/shard_map/while/body/eval_jaxpr/reshape | solution.py:65
  162.7 1.9 copy.88
  164.7 16.6 %bitcast_multiply_fusion.5 = (f32[2048,256]{1,0:T(8,128)}, f32[2048,256]{1,0:T(8,128)}, f32[2048,256]{1,0:T(8,128)}, f32[2048,256]{1,0:T(8,128)}) fusion(f32[2048,256]{1,0:T(8,128)S(1)} %copy.88, f32[32,256]{1,0:T(8,128)S(1)} %copy.89, f32[32,256]{1,0:T(8,128)S(1)} %copy.90), kind=kLoop, calls=%fused_computation.3.clone.1 | loop fusion | flops 3670016 | bytes 10551296 | tf_op jit(solution)/shard_map/while/body/eval_jaxpr/mul | solution.py:71
  181.4 2.0 multiply_add_fusion.2
  183.5 2.4 add.294
  185.9 0.9 sub.75
  186.9 9.8 %fusion.57 = f32[2048,512]{1,0:T(8,128)} fusion(f32[2048,256]{1,0:T(8,128)} %get-tuple-element.193, f32[2048,256]{1,0:T(8,128)} %get-tuple-element.194, f32[256,256]{0,1:T(8,128)S(1)} %bitcast.82, f32[256,256]{0,1:T(8,128)S(1)} %bitcast_negate_fusion.2, f32[256,256]{0,1:T(8,128)S(1)} %bitcast.80), kind=kOutput, calls=%fused_computation.8.clone.1 | convolution fusion | flops 6444285952 | bytes 9175040 | tf_op jit(solution)/shard_map/while/body/eval_jaxpr/dot_general | solution.py:72
  197.0 4.4 %fusion.58 = f32[2048,3]{0,1:T(4,128)S(1)} fusion(f32[2048,512]{1,0:T(8,128)} %fusion.57, f32[256,1]{0,1:T(1,128)S(1)} %tile.19, f32[256,1]{0,1:T(1,128)S(1)} %reshape.240, f32[3]{0:T(128)S(1)} %pad.6.clone.2), kind=kOutput, calls=%fused_computation.16.clone.1 | convolution fusion | flops 20448768 | bytes 4220940 | tf_op jit(solution)/shard_map/while/body/eval_jaxpr/dot_general | solution.py:74
  201.4 8.5 %fusion.55 = f32[2048,512]{1,0:T(8,128)S(1)} fusion(f32[2048,256]{1,0:T(8,128)} %get-tuple-element.187, f32[2048,256]{1,0:T(8,128)S(1)} %copy-done, f32[256,256]{0,1:T(8,128)S(1)} %bitcast.83, f32[256,256]{0,1:T(8,128)S(1)} %bitcast_negate_fusion.2, f32[256,256]{0,1:T(8,128)S(1)} %bitcast.81), kind=kOutput, calls=%fused_computation.4.clone.1 | convolution fusion | flops 6444285952 | bytes 9175040 | tf_op jit(solution)/shard_map/while/body/eval_jaxpr/dot_general | solution.py:72
  209.8 2.0 fusion.56
  213.0 19.1 %collective-permute-start.4 = (bf16[128,2,32]{0,2,1:T(8,128)(2,1)S(1)}, bf16[128,2,32]{0,2,1:T(8,128)(2,1)S(1)}, u32[]{:S(2)}, u32[]{:S(2)}) collective-permute-start(bf16[128,2,32]{0,2,1:T(8,128)(2,1)S(1)} %reshape.212), channel_id=1, source_target_pairs={{0,1},{1,2},{2,3},{3,4},{4,5},{5,6},{6,7},{7,8},{8,9},{9,10},{10,1... | collective-permute-start | bytes 49160 | tf_op jit(solution)/shard_map/ppermute | solution.py:19
  232.9 2.5 collective-permute-start.6
  235.4 2.5 collective-permute-start.7
  239.4 4.4 %collective-permute-start.9 = (bf16[128,2,32]{0,2,1:T(8,128)(2,1)S(1)}, bf16[128,2,32]{0,2,1:T(8,128)(2,1)S(1)}, u32[]{:S(2)}, u32[]{:S(2)}) collective-permute-start(bf16[128,2,32]{0,2,1:T(8,128)(2,1)S(1)} %collective-permute-done.7), channel_id=1, source_target_pairs={{0,15},{1,0},{2,1},{3,2},{4,3},{5,4},{6,5},{7,6},{8,7},{9,8},{10,9... | collective-permute-start | bytes 49160 | tf_op jit(solution)/shard_map/ppermute | solution.py:22
  243.8 0.9 collective-permute-done.8
  245.3 4.4 %collective-permute-start.11 = (bf16[128,2,32]{0,2,1:T(8,128)(2,1)S(1)}, bf16[128,2,32]{0,2,1:T(8,128)(2,1)S(1)}, u32[]{:S(2)}, u32[]{:S(2)}) collective-permute-start(bf16[128,2,32]{0,2,1:T(8,128)(2,1)S(1)} %collective-permute-done.9), channel_id=1, source_target_pairs={{0,15},{1,0},{2,1},{3,2},{4,3},{5,4},{6,5},{7,6},{8,7},{9,8},{10,9... | collective-permute-start | bytes 49160 | tf_op jit(solution)/shard_map/ppermute | solution.py:22
  249.7 0.9 collective-permute-done.10
  251.1 4.4 %collective-permute-start.13 = (bf16[128,2,32]{0,2,1:T(8,128)(2,1)S(1)}, bf16[128,2,32]{0,2,1:T(8,128)(2,1)S(1)}, u32[]{:S(2)}, u32[]{:S(2)}) collective-permute-start(bf16[128,2,32]{0,2,1:T(8,128)(2,1)S(1)} %collective-permute-done.11), channel_id=1, source_target_pairs={{0,15},{1,0},{2,1},{3,2},{4,3},{5,4},{6,5},{7,6},{8,7},{9,8},{10,9... | collective-permute-start | bytes 49160 | tf_op jit(solution)/shard_map/ppermute | solution.py:22
  255.5 0.9 collective-permute-done.12
  257.0 4.4 %collective-permute-start.15 = (bf16[128,2,32]{0,2,1:T(8,128)(2,1)S(1)}, bf16[128,2,32]{0,2,1:T(8,128)(2,1)S(1)}, u32[]{:S(2)}, u32[]{:S(2)}) collective-permute-start(bf16[128,2,32]{0,2,1:T(8,128)(2,1)S(1)} %collective-permute-done.13), channel_id=1, source_target_pairs={{0,15},{1,0},{2,1},{3,2},{4,3},{5,4},{6,5},{7,6},{8,7},{9,8},{10,9... | collective-permute-start | bytes 49160 | tf_op jit(solution)/shard_map/ppermute | solution.py:22
  262.9 4.4 %collective-permute-start.17 = (bf16[128,2,32]{0,2,1:T(8,128)(2,1)S(1)}, bf16[128,2,32]{0,2,1:T(8,128)(2,1)S(1)}, u32[]{:S(2)}, u32[]{:S(2)}) collective-permute-start(bf16[128,2,32]{0,2,1:T(8,128)(2,1)S(1)} %collective-permute-done.15), channel_id=1, source_target_pairs={{0,15},{1,0},{2,1},{3,2},{4,3},{5,4},{6,5},{7,6},{8,7},{9,8},{10,9... | collective-permute-start | bytes 49160 | tf_op jit(solution)/shard_map/ppermute | solution.py:22
  280.3 0.9 copy.78
  (116 shorter events, 21.0 us)
Async XLA Ops:
  0.0 7.7 %copy-start.3 = (s32[128,72]{0,1:T(8,128)S(1)}, s32[128,72]{0,1:T(8,128)}, u32[]{:S(2)}) copy-start(s32[128,72]{0,1:T(8,128)} %param.8) | copy-start | bytes 110596
  0.0 7.7 %copy-start.4 = (f32[72]{0:T(128)S(1)}, f32[72]{0:T(128)}, u32[]{:S(2)}) copy-start(f32[72]{0:T(128)} %param.9) | copy-start | bytes 868
  2.9 12.4 %copy-start.5 = (s32[32]{0:T(128)S(1)}, s32[32]{0:T(128)}, u32[]{:S(2)}) copy-start(s32[32]{0:T(128)} %param.13) | copy-start | bytes 388
  2.9 12.4 %collective-permute-start.1 = (bf16[72,8192]{1,0:T(8,128)(2,1)}, bf16[72,8192]{1,0:T(8,128)(2,1)}, u32[]{:S(2)}, u32[]{:S(2)}) collective-permute-start(bf16[72,8192]{1,0:T(8,128)(2,1)} %get-tuple-element.136), channel_id=1, source_target_pairs={{0,1},{1,2},{2,3},{3,4},{4,5},{5,6},{6,7},{7,8},{8,9},{9,10},{10,1... | collective-permute-start | bytes 3538952 | tf_op jit(solution)/shard_map/ppermute | solution.py:32
  6.4 10.9 %collective-permute-start.3 = (bf16[72,8192]{1,0:T(8,128)(2,1)S(1)}, bf16[72,8192]{1,0:T(8,128)(2,1)}, u32[]{:S(2)}, u32[]{:S(2)}) collective-permute-start(bf16[72,8192]{1,0:T(8,128)(2,1)S(1)} %get-tuple-element.137), channel_id=1, source_target_pairs={{1,0},{2,1},{3,2},{4,3},{5,4},{6,5},{7,6},{8,7},{9,8},{10,9},{11,1... | collective-permute-start | bytes 3538952 | tf_op jit(solution)/shard_map/ppermute | solution.py:32
  7.8 7.5 %collective-permute-start = (bf16[128,72]{0,1:T(8,128)(2,1)S(1)}, bf16[128,72]{0,1:T(8,128)(2,1)S(1)}, u32[]{:S(2)}, u32[]{:S(2)}) collective-permute-start(bf16[128,72]{0,1:T(8,128)(2,1)S(1)} %multiply_convert_fusion), channel_id=1, source_target_pairs={{0,1},{1,2},{2,3},{3,4},{4,5},{5,6},{6,7},{7,8},{8,9},{9,10},{10,1... | collective-permute-start | bytes 55304 | tf_op jit(solution)/shard_map/ppermute | solution.py:32
  12.0 5.4 %collective-permute-start.2 = (bf16[128,72]{0,1:T(8,128)(2,1)S(1)}, bf16[128,72]{0,1:T(8,128)(2,1)S(1)}, u32[]{:S(2)}, u32[]{:S(2)}) collective-permute-start(bf16[128,72]{0,1:T(8,128)(2,1)S(1)} %multiply_convert_fusion), channel_id=1, source_target_pairs={{1,0},{2,1},{3,2},{4,3},{5,4},{6,5},{7,6},{8,7},{9,8},{10,9},{11,1... | collective-permute-start | bytes 55304 | tf_op jit(solution)/shard_map/ppermute | solution.py:32
  27.8 9.3 %copy-start.1 = (f32[32,16,16]{0,2,1:T(8,128)S(1)}, f32[32,16,16]{0,2,1:T(8,128)}, u32[]{:S(2)}) copy-start(f32[32,16,16]{0,2,1:T(8,128)} %param.11) | copy-start | bytes 98308
  27.8 9.3 %copy-start.2 = (f32[32,16,16]{0,2,1:T(8,128)S(1)}, f32[32,16,16]{0,2,1:T(8,128)}, u32[]{:S(2)}) copy-start(f32[32,16,16]{0,2,1:T(8,128)} %param.12) | copy-start | bytes 98308
  117.1 4.7 %copy-start = (f32[2048,256]{1,0:T(8,128)S(1)}, f32[2048,256]{1,0:T(8,128)}, u32[]{:S(2)}) copy-start(f32[2048,256]{1,0:T(8,128)} %get-tuple-element.188) | copy-start | bytes 6291460 | tf_op jit(solution)/shard_map/while
  196.7 4.7 %copy-start = (f32[2048,256]{1,0:T(8,128)S(1)}, f32[2048,256]{1,0:T(8,128)}, u32[]{:S(2)}) copy-start(f32[2048,256]{1,0:T(8,128)} %get-tuple-element.188) | copy-start | bytes 6291460 | tf_op jit(solution)/shard_map/while
  213.0 20.0 %collective-permute-start.4 = (bf16[128,2,32]{0,2,1:T(8,128)(2,1)S(1)}, bf16[128,2,32]{0,2,1:T(8,128)(2,1)S(1)}, u32[]{:S(2)}, u32[]{:S(2)}) collective-permute-start(bf16[128,2,32]{0,2,1:T(8,128)(2,1)S(1)} %reshape.212), channel_id=1, source_target_pairs={{0,1},{1,2},{2,3},{3,4},{4,5},{5,6},{6,7},{7,8},{8,9},{9,10},{10,1... | collective-permute-start | bytes 49160 | tf_op jit(solution)/shard_map/ppermute | solution.py:19
  232.1 3.3 %collective-permute-start.5 = (bf16[128,2,32]{0,2,1:T(8,128)(2,1)S(1)}, bf16[128,2,32]{0,2,1:T(8,128)(2,1)S(1)}, u32[]{:S(2)}, u32[]{:S(2)}) collective-permute-start(bf16[128,2,32]{0,2,1:T(8,128)(2,1)S(1)} %reshape.212), channel_id=1, source_target_pairs={{0,15},{1,0},{2,1},{3,2},{4,3},{5,4},{6,5},{7,6},{8,7},{9,8},{10,9... | collective-permute-start | bytes 49160 | tf_op jit(solution)/shard_map/ppermute | solution.py:22
  232.9 5.9 %collective-permute-start.6 = (bf16[128,2,32]{0,2,1:T(8,128)(2,1)S(1)}, bf16[128,2,32]{0,2,1:T(8,128)(2,1)S(1)}, u32[]{:S(2)}, u32[]{:S(2)}) collective-permute-start(bf16[128,2,32]{0,2,1:T(8,128)(2,1)S(1)} %collective-permute-done.4), channel_id=1, source_target_pairs={{0,1},{1,2},{2,3},{3,4},{4,5},{5,6},{6,7},{7,8},{8,9},{9,10},{10,1... | collective-permute-start | bytes 49160 | tf_op jit(solution)/shard_map/ppermute | solution.py:19
  235.4 4.0 %collective-permute-start.7 = (bf16[128,2,32]{0,2,1:T(8,128)(2,1)S(1)}, bf16[128,2,32]{0,2,1:T(8,128)(2,1)S(1)}, u32[]{:S(2)}, u32[]{:S(2)}) collective-permute-start(bf16[128,2,32]{0,2,1:T(8,128)(2,1)S(1)} %collective-permute-done.5), channel_id=1, source_target_pairs={{0,15},{1,0},{2,1},{3,2},{4,3},{5,4},{6,5},{7,6},{8,7},{9,8},{10,9... | collective-permute-start | bytes 49160 | tf_op jit(solution)/shard_map/ppermute | solution.py:22
  238.8 5.9 %collective-permute-start.8 = (bf16[128,2,32]{0,2,1:T(8,128)(2,1)S(1)}, bf16[128,2,32]{0,2,1:T(8,128)(2,1)S(1)}, u32[]{:S(2)}, u32[]{:S(2)}) collective-permute-start(bf16[128,2,32]{0,2,1:T(8,128)(2,1)S(1)} %collective-permute-done.6), channel_id=1, source_target_pairs={{0,1},{1,2},{2,3},{3,4},{4,5},{5,6},{6,7},{7,8},{8,9},{9,10},{10,1... | collective-permute-start | bytes 49160 | tf_op jit(solution)/shard_map/ppermute | solution.py:19
  239.4 5.9 %collective-permute-start.9 = (bf16[128,2,32]{0,2,1:T(8,128)(2,1)S(1)}, bf16[128,2,32]{0,2,1:T(8,128)(2,1)S(1)}, u32[]{:S(2)}, u32[]{:S(2)}) collective-permute-start(bf16[128,2,32]{0,2,1:T(8,128)(2,1)S(1)} %collective-permute-done.7), channel_id=1, source_target_pairs={{0,15},{1,0},{2,1},{3,2},{4,3},{5,4},{6,5},{7,6},{8,7},{9,8},{10,9... | collective-permute-start | bytes 49160 | tf_op jit(solution)/shard_map/ppermute | solution.py:22
  244.7 5.9 %collective-permute-start.10 = (bf16[128,2,32]{0,2,1:T(8,128)(2,1)S(1)}, bf16[128,2,32]{0,2,1:T(8,128)(2,1)S(1)}, u32[]{:S(2)}, u32[]{:S(2)}) collective-permute-start(bf16[128,2,32]{0,2,1:T(8,128)(2,1)S(1)} %collective-permute-done.8), channel_id=1, source_target_pairs={{0,1},{1,2},{2,3},{3,4},{4,5},{5,6},{6,7},{7,8},{8,9},{9,10},{10,1... | collective-permute-start | bytes 49160 | tf_op jit(solution)/shard_map/ppermute | solution.py:19
  245.3 5.9 %collective-permute-start.11 = (bf16[128,2,32]{0,2,1:T(8,128)(2,1)S(1)}, bf16[128,2,32]{0,2,1:T(8,128)(2,1)S(1)}, u32[]{:S(2)}, u32[]{:S(2)}) collective-permute-start(bf16[128,2,32]{0,2,1:T(8,128)(2,1)S(1)} %collective-permute-done.9), channel_id=1, source_target_pairs={{0,15},{1,0},{2,1},{3,2},{4,3},{5,4},{6,5},{7,6},{8,7},{9,8},{10,9... | collective-permute-start | bytes 49160 | tf_op jit(solution)/shard_map/ppermute | solution.py:22
  250.6 5.9 %collective-permute-start.12 = (bf16[128,2,32]{0,2,1:T(8,128)(2,1)S(1)}, bf16[128,2,32]{0,2,1:T(8,128)(2,1)S(1)}, u32[]{:S(2)}, u32[]{:S(2)}) collective-permute-start(bf16[128,2,32]{0,2,1:T(8,128)(2,1)S(1)} %collective-permute-done.10), channel_id=1, source_target_pairs={{0,1},{1,2},{2,3},{3,4},{4,5},{5,6},{6,7},{7,8},{8,9},{9,10},{10,1... | collective-permute-start | bytes 49160 | tf_op jit(solution)/shard_map/ppermute | solution.py:19
  251.1 5.9 %collective-permute-start.13 = (bf16[128,2,32]{0,2,1:T(8,128)(2,1)S(1)}, bf16[128,2,32]{0,2,1:T(8,128)(2,1)S(1)}, u32[]{:S(2)}, u32[]{:S(2)}) collective-permute-start(bf16[128,2,32]{0,2,1:T(8,128)(2,1)S(1)} %collective-permute-done.11), channel_id=1, source_target_pairs={{0,15},{1,0},{2,1},{3,2},{4,3},{5,4},{6,5},{7,6},{8,7},{9,8},{10,9... | collective-permute-start | bytes 49160 | tf_op jit(solution)/shard_map/ppermute | solution.py:22
  256.4 5.9 %collective-permute-start.14 = (bf16[128,2,32]{0,2,1:T(8,128)(2,1)S(1)}, bf16[128,2,32]{0,2,1:T(8,128)(2,1)S(1)}, u32[]{:S(2)}, u32[]{:S(2)}) collective-permute-start(bf16[128,2,32]{0,2,1:T(8,128)(2,1)S(1)} %collective-permute-done.12), channel_id=1, source_target_pairs={{0,1},{1,2},{2,3},{3,4},{4,5},{5,6},{6,7},{7,8},{8,9},{9,10},{10,1... | collective-permute-start | bytes 49160 | tf_op jit(solution)/shard_map/ppermute | solution.py:19
  257.0 5.9 %collective-permute-start.15 = (bf16[128,2,32]{0,2,1:T(8,128)(2,1)S(1)}, bf16[128,2,32]{0,2,1:T(8,128)(2,1)S(1)}, u32[]{:S(2)}, u32[]{:S(2)}) collective-permute-start(bf16[128,2,32]{0,2,1:T(8,128)(2,1)S(1)} %collective-permute-done.13), channel_id=1, source_target_pairs={{0,15},{1,0},{2,1},{3,2},{4,3},{5,4},{6,5},{7,6},{8,7},{9,8},{10,9... | collective-permute-start | bytes 49160 | tf_op jit(solution)/shard_map/ppermute | solution.py:22
  262.3 5.9 %collective-permute-start.16 = (bf16[128,2,32]{0,2,1:T(8,128)(2,1)S(1)}, bf16[128,2,32]{0,2,1:T(8,128)(2,1)S(1)}, u32[]{:S(2)}, u32[]{:S(2)}) collective-permute-start(bf16[128,2,32]{0,2,1:T(8,128)(2,1)S(1)} %collective-permute-done.14), channel_id=1, source_target_pairs={{0,1},{1,2},{2,3},{3,4},{4,5},{5,6},{6,7},{7,8},{8,9},{9,10},{10,1... | collective-permute-start | bytes 49160 | tf_op jit(solution)/shard_map/ppermute | solution.py:19
  262.9 15.9 %collective-permute-start.17 = (bf16[128,2,32]{0,2,1:T(8,128)(2,1)S(1)}, bf16[128,2,32]{0,2,1:T(8,128)(2,1)S(1)}, u32[]{:S(2)}, u32[]{:S(2)}) collective-permute-start(bf16[128,2,32]{0,2,1:T(8,128)(2,1)S(1)} %collective-permute-done.15), channel_id=1, source_target_pairs={{0,15},{1,0},{2,1},{3,2},{4,3},{5,4},{6,5},{7,6},{8,7},{9,8},{10,9... | collective-permute-start | bytes 49160 | tf_op jit(solution)/shard_map/ppermute | solution.py:22
  268.2 11.5 %collective-permute-start.18 = (bf16[128,2,32]{0,2,1:T(8,128)(2,1)S(1)}, bf16[128,2,32]{0,2,1:T(8,128)(2,1)S(1)}, u32[]{:S(2)}, u32[]{:S(2)}) collective-permute-start(bf16[128,2,32]{0,2,1:T(8,128)(2,1)S(1)} %collective-permute-done.16), channel_id=1, source_target_pairs={{0,1},{1,2},{2,3},{3,4},{4,5},{5,6},{6,7},{7,8},{8,9},{9,10},{10,1... | collective-permute-start | bytes 49160 | tf_op jit(solution)/shard_map/ppermute | solution.py:19
